TPU v7x, 32 devices: a whole 2x2x4 slice. The times are simulated.
32 devices in a mesh: groups: 2 (over x), section: 8 (over z, y), head: 2 (over core).
Axes of the slice: x: 2, y: 2, z: 4, core: 2. Of those that a mesh axis runs over, the one named last changes fastest.
Arguments:
- video_tokens: bfloat16 [8192, 1536], P(('groups', 'section', 'head')), parts along dimension 0, may hold values from -6 to 6
- modulation: float32 [6, 1536], P('groups'), parts along dimension 0, may hold values from -3 to 3
- project_weight: bfloat16 [3, 1536, 1536], P(None, None, 'head'), may hold values from -0.15625 to 0.15625
- output_weight: bfloat16 [1536, 1536], P('head'), may hold values from -0.15625 to 0.15625
- norm_gains: float32 [3, 128], replicated, may hold values from 1 to 2
- text_cache: bfloat16 [2, 512, 1536], P(None, 'groups', 'head'), parts along dimension 1, may hold values from -6 to 6
- text_count: int32 [2], P('groups'), parts along dimension 0, may hold values from 1 to 256, as said below
- video_keep: int32 [8192], P('groups'), parts along dimension 0, may hold values 0 or 1
- patch_order: int32 [16], P('groups'), parts along dimension 0, may hold values from 0 to 7, each once
- stale_cache: bfloat16 [2, 8192, 1536], P(None, ('groups', 'section'), 'head'), parts along dimension 1, may hold values from -6 to 6
Outputs:
- updated: bfloat16 [8192, 1536], P(('groups', 'section', 'head')), parts along dimension 0
- fresh_cache: bfloat16 [2, 8192, 1536], P(None, ('groups', 'section'), 'head'), parts along dimension 1
There are 2 independent parts, one for each index of `groups`. A program takes and returns all parts, laid end to end along the dimension named above; an argument that names none is the same for every part. Nothing has to cross between parts.
Inputs may be any that keep to these rules, and one draw needn't show every extreme that they name: The first text_count text tokens are real, the rest are padding. `video_keep`: 1 keeps a video token as a key, 0 marks padding. `patch_order`: each place 0 to 7 is held by exactly one patch.
All inputs are finite; a program needn't handle non-finite values.
Results may differ from a plain program's by a relative error of at most 0.0049.
Values may be sent and summed in bfloat16 or wider, within the bound.
A program may use at most 128 MiB of HBM per device.

v0:
```python
import jax
import jax.numpy as jnp
from jax import lax
from jax.experimental import pallas as pl
from jax.experimental.pallas import tpu as pltpu
from jax.sharding import PartitionSpec as P

epsilon = 1e-06
log2_e = 1.4426950408889634
MESH = pl.DeviceIdType.MESH
f32 = jnp.float32
bf16 = jnp.bfloat16


def dot_nt(a, b):
    return lax.dot_general(a, b, (((1,), (1,)), ((), ())), preferred_element_type=f32)


def head_norm(rows, gain):
    return rows * lax.rsqrt(jnp.mean(rows * rows, axis=-1, keepdims=True) + epsilon) * gain


def kernel(
    order_ref,
    count_ref,
    tokens_hbm,
    modulation_hbm,
    gains_hbm,
    keep_hbm,
    weight_hbm,
    output_weight_hbm,
    text_hbm,
    stale_hbm,
    updated_ref,
    raw,
    tokens_ref,
    modulation_ref,
    gains_ref,
    keep_ref,
    weight,
    output_weight,
    text,
    stale,
    normed,
    query,
    query_mate,
    query_far,
    keys,
    values,
    text_keys,
    text_values,
    own_sum,
    mate_sum,
    far_out,
    far_total_out,
    far_in,
    far_total_in,
    back_out,
    back_total_out,
    back_in,
    back_total_in,
    attended,
    mixed_out,
    mixed_in,
    partial,
    load_sem,
    normed_sem,
    query_sem,
    forward_sem,
    far_sem,
    far_total_sem,
    back_sem,
    back_total_sem,
    mixed_sem,
):
    count = lax.axis_size("section")
    me = lax.axis_index("section")
    core = lax.axis_index("head")
    other_core = 1 - core
    parity = lax.rem(me, 2)
    mate = me + 1 - 2 * parity
    step = 2 - 4 * parity
    ahead = me + step
    behind = me - step
    has_ahead = jnp.logical_and(ahead >= 0, ahead < count)
    has_behind = jnp.logical_and(behind >= 0, behind < count)
    rows = tokens_hbm.shape[0]
    head = gains_ref.shape[1]
    width = weight.shape[2]
    heads = width // head
    units = 2 * heads
    patch = 2 * rows

    loads = [
        pltpu.make_async_copy(weight_hbm.at[c], weight.at[c], load_sem.at[c]) for c in range(3)
    ]
    loads.append(pltpu.make_async_copy(stale_hbm, stale, load_sem.at[3]))
    loads.append(pltpu.make_async_copy(text_hbm, text, load_sem.at[4]))
    loads.append(pltpu.make_async_copy(output_weight_hbm, output_weight, load_sem.at[5]))
    small = [
        pltpu.make_async_copy(source, target, load_sem.at[6 + place])
        for place, (source, target) in enumerate(
            (
                (tokens_hbm, tokens_ref),
                (modulation_hbm, modulation_ref),
                (gains_hbm, gains_ref),
                (keep_hbm, keep_ref),
            )
        )
    ]
    for load in small:
        load.start()
    loads[0].start()

    barrier = pltpu.get_barrier_semaphore()
    pl.semaphore_signal(barrier, inc=1, device_id={"head": other_core}, device_id_type=MESH)
    pl.semaphore_signal(barrier, inc=1, device_id={"section": mate}, device_id_type=MESH)

    @pl.when(has_ahead)
    def _():
        pl.semaphore_signal(barrier, inc=1, device_id={"section": ahead}, device_id_type=MESH)

    @pl.when(has_behind)
    def _():
        pl.semaphore_signal(barrier, inc=1, device_id={"section": behind}, device_id_type=MESH)

    for load in small:
        load.wait()
    hidden = tokens_ref[...].astype(f32)
    shifted = hidden - jnp.mean(hidden, axis=-1, keepdims=True)
    spread = jnp.mean(shifted * shifted, axis=-1, keepdims=True)
    normed[0] = (
        shifted * lax.rsqrt(spread + epsilon) * (1.0 + modulation_ref[1:2, :])
        + modulation_ref[0:1, :]
    ).astype(bf16)

    pl.semaphore_wait(
        barrier, 2 + has_ahead.astype(jnp.int32) + has_behind.astype(jnp.int32)
    )

    normed_copy = pltpu.make_async_remote_copy(
        src_ref=normed.at[0],
        dst_ref=normed.at[1],
        send_sem=normed_sem.at[0],
        recv_sem=normed_sem.at[1],
        device_id={"head": other_core},
        device_id_type=MESH,
    )
    normed_copy.start()

    def remote(source, target, sems, unit, device):
        return pltpu.make_async_remote_copy(
            src_ref=source.at[unit],
            dst_ref=target.at[unit],
            send_sem=sems.at[0, unit],
            recv_sem=sems.at[1, unit],
            device_id={"section": device},
            device_id_type=MESH,
        )

    def query_copy(unit):
        return remote(query, query_mate, query_sem, unit, mate)

    def forward_copy(unit, device):
        return remote(query_mate, query_far, forward_sem, unit, device)

    def far_copies(unit, device):
        return (
            remote(far_out, far_in, far_sem, unit, device),
            remote(far_total_out, far_total_in, far_total_sem, unit, device),
        )

    def back_copies(unit):
        return (
            remote(back_out, back_in, back_sem, unit, mate),
            remote(back_total_out, back_total_in, back_total_sem, unit, mate),
        )

    factor = head ** (-0.5) * log2_e
    pair = 2 if heads % 2 == 0 else 1
    span = pair * head

    def columns(step_index):
        return pl.ds(pl.multiple_of(step_index * span, span), span)

    def project_queries(half):
        @pl.loop(0, heads // pair)
        def _(c):
            part = jnp.dot(normed[half], weight[0, :, columns(c)], preferred_element_type=f32)
            for j in range(pair):
                unit = half * heads + c * pair + j
                query[unit] = (
                    head_norm(part[:, j * head : (j + 1) * head], gains_ref[0:1, :]) * factor
                ).astype(bf16)
                query_copy(unit).start()

    early = min(3, heads)

    def forward(unit):
        query_copy(unit).wait_recv()

        @pl.when(has_ahead)
        def _():
            forward_copy(unit, ahead).start()

    for load in loads[1:]:
        load.start()
    loads[0].wait()
    project_queries(0)
    normed_copy.wait_recv()
    project_queries(1)
    loads[1].wait()
    loads[2].wait()
    own_rows = pl.ds(pl.multiple_of(core * rows, rows), rows)
    other_rows = pl.ds(pl.multiple_of(other_core * rows, rows), rows)

    @pl.loop(0, heads // pair)
    def _(c):
        for w in range(2):
            part = jnp.dot(
                normed[...].reshape(patch, normed.shape[2]),
                weight[1 + w, :, columns(c)],
                preferred_element_type=f32,
            ).astype(bf16)
            raw[w, own_rows, columns(c)] = part[0:rows]
            raw[w, other_rows, columns(c)] = part[rows:patch]

        @pl.when(c < early)
        def _():
            forward(c)

    @pl.loop(min(early, heads // pair), early)
    def _(i):
        forward(i)

    loads[3].wait()
    loads[4].wait()

    keep_row = keep_ref[pl.ds(pl.multiple_of(me * patch, patch), patch)].astype(f32)
    keep = jnp.transpose(jnp.broadcast_to(keep_row[None, :], (head, patch)))
    text_rows = text.shape[1]
    live = (
        lax.broadcasted_iota(jnp.int32, (text_rows, head), 0) < count_ref[0]
    ).astype(f32)

    @pl.loop(0, heads)
    def _(h):
        lanes = pl.ds(pl.multiple_of(h * head, head), head)
        for version, cache in ((0, raw), (1, stale)):
            keys[version, h] = head_norm(
                cache[0, :, lanes].astype(f32), gains_ref[1:2, :]
            ).astype(bf16)
            values[version, h, :, 0:head] = (cache[1, :, lanes].astype(f32) * keep).astype(bf16)
            values[version, h, :, head : 2 * head] = keep.astype(bf16)
        text_keys[h] = head_norm(text[0, :, lanes].astype(f32), gains_ref[2:3, :]).astype(bf16)
        text_values[h, :, 0:head] = (text[1, :, lanes].astype(f32) * live).astype(bf16)
        text_values[h, :, head : 2 * head] = live.astype(bf16)

    own_slot = order_ref[me]
    mate_version = jnp.where(own_slot < order_ref[mate], 0, 1)
    far_patch = jnp.clip(me - 1 + 2 * parity, 0, count - 1)
    far_version = jnp.where(own_slot < order_ref[far_patch], 0, 1)

    def weighted(queries, key_rows, value_rows):
        weights = jnp.exp2(dot_nt(queries, key_rows)).astype(bf16)
        return jnp.dot(weights, value_rows, preferred_element_type=f32)

    def total_rows(summed):
        return jnp.transpose(summed[:, head : 2 * head])[0:1, :]

    def send_back(unit):
        numerator = mate_sum[unit, :, 0:head]
        totals = total_rows(mate_sum[unit])

        @pl.when(has_ahead)
        def _():
            for copy in far_copies(unit, mate):
                copy.wait_recv()
            back_out[unit] = (numerator + far_in[unit].astype(f32)).astype(bf16)
            back_total_out[unit] = totals + far_total_in[unit]

        @pl.when(jnp.logical_not(has_ahead))
        def _():
            back_out[unit] = numerator.astype(bf16)
            back_total_out[unit] = totals

        for copy in back_copies(unit):
            copy.start()

    ahead_backs = min(2, heads)

    @pl.loop(early, units + 2 * early)
    def _(i):
        @pl.when(i < units)
        def _():
            forward(i)

        unit = i - early

        @pl.when(unit < units)
        def _():
            h = lax.rem(unit, heads)

            @pl.when(has_behind)
            def _():
                forward_copy(unit, mate).wait_recv()
                summed = weighted(query_far[unit], keys[far_version, h], values[far_version, h])
                far_out[unit] = summed[:, 0:head].astype(bf16)
                far_total_out[unit] = total_rows(summed)
                for copy in far_copies(unit, behind):
                    copy.start()

            mate_sum[unit] = weighted(
                query_mate[unit], keys[mate_version, h], values[mate_version, h]
            )
            own_sum[unit] = weighted(query[unit], keys[0, h], values[0, h]) + weighted(
                query[unit], text_keys[h], text_values[h]
            )

        @pl.when(jnp.logical_and(i >= units - ahead_backs, i < units))
        def _():
            send_back(i - units + ahead_backs)

        @pl.when(i >= heads + 2 * early)
        def _():
            send_back(i - 2 * early)

    @pl.loop(ahead_backs, heads)
    def _(i):
        send_back(i)

    def gather_range(half, first, last):
        @pl.loop(first, last)
        def _(h):
            unit = half * heads + h
            for copy in back_copies(unit):
                copy.wait_recv()
            total = jnp.transpose(
                jnp.broadcast_to(back_total_in[unit], (head, rows))
            )
            mine = own_sum[unit]
            attended[half, :, pl.ds(pl.multiple_of(h * head, head), head)] = (
                (mine[:, 0:head] + back_in[unit].astype(f32))
                / (mine[:, head : 2 * head] + total)
            ).astype(bf16)

    mixed_copy = pltpu.make_async_remote_copy(
        src_ref=mixed_out,
        dst_ref=mixed_in,
        send_sem=mixed_sem.at[0],
        recv_sem=mixed_sem.at[1],
        device_id={"head": other_core},
        device_id_type=MESH,
    )
    full = output_weight.shape[1]
    wide = 512 if full % 512 == 0 else full

    gather_range(1, 0, heads)
    loads[5].wait()

    @pl.loop(0, full // wide)
    def _(c):
        here = pl.ds(pl.multiple_of(c * wide, wide), wide)
        mixed_out[:, here] = jnp.dot(
            attended[1], output_weight[:, here], preferred_element_type=f32
        ).astype(bf16)

    mixed_copy.start()
    split = heads - min(2, heads - 1)
    gather_range(0, 0, split)

    @pl.loop(0, full // wide)
    def _(c):
        here = pl.ds(pl.multiple_of(c * wide, wide), wide)
        partial[:, here] = jnp.dot(
            attended[0, :, 0 : split * head],
            output_weight[0 : split * head, here],
            preferred_element_type=f32,
        )

    mixed_copy.wait_recv()

    @pl.loop(0, full // wide)
    def _(c):
        here = pl.ds(pl.multiple_of(c * wide, wide), wide)
        partial[:, here] = partial[:, here] + mixed_in[:, here].astype(f32)

    gather_range(0, split, heads)

    @pl.loop(0, full // wide)
    def _(c):
        here = pl.ds(pl.multiple_of(c * wide, wide), wide)
        mixed = partial[:, here] + jnp.dot(
            attended[0, :, split * head :],
            output_weight[split * head :, here],
            preferred_element_type=f32,
        )
        updated_ref[:, here] = (
            tokens_ref[:, here].astype(f32) + modulation_ref[2:3, here] * mixed
        ).astype(bf16)

    normed_copy.wait_send()
    mixed_copy.wait_send()

    @pl.loop(0, units)
    def _(i):
        query_copy(i).wait_send()
        for copy in back_copies(i):
            copy.wait_send()

        @pl.when(has_ahead)
        def _():
            forward_copy(i, mate).wait_send()

        @pl.when(has_behind)
        def _():
            for copy in far_copies(i, mate):
                copy.wait_send()


def on_device(
    video_tokens,
    modulation,
    project_weight,
    output_weight,
    norm_gains,
    text_cache,
    text_count,
    video_keep,
    patch_order,
    stale_cache,
):
    head = norm_gains.shape[1]
    rows, model = video_tokens.shape
    width = project_weight.shape[2]
    patch = stale_cache.shape[1]
    text_rows = text_cache.shape[1]
    heads = width // head
    units = 2 * heads
    smem = pl.BlockSpec(memory_space=pltpu.SMEM)
    vmem = pl.BlockSpec(memory_space=pltpu.VMEM)
    hbm = pl.BlockSpec(memory_space=pl.ANY)
    unit_rows = pltpu.VMEM((units, rows, head), bf16)
    unit_totals = pltpu.VMEM((units, 1, rows), f32)
    unit_sums = pltpu.VMEM((units, rows, 2 * head), f32)
    unit_sems = pltpu.SemaphoreType.DMA((2, units))
    return pl.pallas_call(
        kernel,
        out_shape=(
            pltpu.VMEM(video_tokens.shape, bf16),
            pltpu.VMEM(stale_cache.shape, bf16),
        ),
        in_specs=[smem, smem] + [hbm] * 8,
        out_specs=(vmem, vmem),
        scratch_shapes=[
            pltpu.VMEM(video_tokens.shape, bf16),
            pltpu.VMEM(modulation.shape, f32),
            pltpu.VMEM(norm_gains.shape, f32),
            pltpu.VMEM(video_keep.shape, jnp.int32),
            pltpu.VMEM(project_weight.shape, bf16),
            pltpu.VMEM(output_weight.shape, bf16),
            pltpu.VMEM(text_cache.shape, bf16),
            pltpu.VMEM(stale_cache.shape, bf16),
            pltpu.VMEM((2, rows, model), bf16),
            unit_rows,
            unit_rows,
            unit_rows,
            pltpu.VMEM((2, heads, patch, head), bf16),
            pltpu.VMEM((2, heads, patch, 2 * head), bf16),
            pltpu.VMEM((heads, text_rows, head), bf16),
            pltpu.VMEM((heads, text_rows, 2 * head), bf16),
            unit_sums,
            unit_sums,
            unit_rows,
            unit_totals,
            unit_rows,
            unit_totals,
            unit_rows,
            unit_totals,
            unit_rows,
            unit_totals,
            pltpu.VMEM((2, rows, width), bf16),
            pltpu.VMEM((rows, model), bf16),
            pltpu.VMEM((rows, model), bf16),
            pltpu.VMEM((rows, model), f32),
            pltpu.SemaphoreType.DMA((10,)),
            pltpu.SemaphoreType.DMA((2,)),
            unit_sems,
            unit_sems,
            unit_sems,
            unit_sems,
            unit_sems,
            unit_sems,
            pltpu.SemaphoreType.DMA((2,)),
        ],
        compiler_params=pltpu.CompilerParams(
            collective_id=0, has_side_effects=True, vmem_limit_bytes=60 * 1024 * 1024
        ),
    )(
        patch_order,
        text_count,
        video_tokens,
        modulation,
        norm_gains,
        video_keep,
        project_weight,
        output_weight,
        text_cache,
        stale_cache,
    )


def solution(mesh):
    placed = (
        P(("groups", "section", "head"), None),
        P("groups", None),
        P(None, None, "head"),
        P("head", None),
        P(),
        P(None, "groups", "head"),
        P("groups"),
        P("groups"),
        P("groups"),
        P(None, ("groups", "section"), "head"),
    )
    return jax.shard_map(
        on_device,
        mesh=mesh,
        in_specs=placed,
        out_specs=(P(("groups", "section", "head"), None), P(None, ("groups", "section"), "head")),
        check_vma=False,
    )
```

profile of v0, /device:TPU:0, one launch (start us, length us, event | category | flops | bytes accessed | tf_op | source)
XLA Modules:
  0.0 49.3 jit_solution(9242026199352450201)
XLA Ops:
  1.3 46.0 %shard_map.113 = (bf16[256,1536]{1,0:T(8,128)(2,1)S(1)}, bf16[2,512,768]{2,1,0:T(8,128)(2,1)S(1)}) custom-call(s32[8]{0:T(128)} %order_ref.1, s32[1]{0:T(128)S(6)} %copy.16.count_ref, bf16[256,1536]{1,0:T(8,128)(2,1)} %tokens_hbm.1, f32[3,1536]{1,0:T(4,128)} %modulation_hbm.1, f32[3,128]{1,0:T(4,128)} %gains_hbm.1, s32[4096]{0:T(1024)} %keep_hbm.1, ...), custom_call_target="tpu_custom_call" | custom-call | tf_op jit(solution)/shard_map/pallas_call | solution.py:447
  47.2 0.9 %copy.14 = bf16[256,1536]{1,0:T(8,128)(2,1)} copy(bf16[256,1536]{1,0:T(8,128)(2,1)S(1)} %get-tuple-element.2) | data formatting | bytes 1572864
  48.1 1.1 %copy.15 = bf16[2,512,768]{2,1,0:T(8,128)(2,1)} copy(bf16[2,512,768]{2,1,0:T(8,128)(2,1)S(1)} %get-tuple-element.3) | data formatting | bytes 3145728
where the time goes:
time: 49.4 us; the launch traced here: 49.3 us
  Pallas kernels  46 us (93%)
  local copies, waits for them, and re-layouts  2.02 us (4%)
  between operations  1.29 us (3%)
    pallas_call x1, Pallas kernels, on_device(): pl.pallas_call(kernel, out_shape=(pltpu.VMEM(video_tokens.shape, bf16), p...  46 us
    unnamed x2, local copies, waits for them, and re-layouts  2.02 us

commit v1 on v0

--- a/solution.py
+++ b/solution.py
@@ -21,8 +21,8 @@
 
 
 def kernel(
-    order_ref,
-    count_ref,
+    order_hbm,
+    count_hbm,
     tokens_hbm,
     modulation_hbm,
     gains_hbm,
@@ -31,10 +31,14 @@
     output_weight_hbm,
     text_hbm,
     stale_hbm,
-    updated_ref,
+    base,
+    last,
+    last_weight,
+    modulation_ref,
     raw,
+    order_ref,
+    count_ref,
     tokens_ref,
-    modulation_ref,
     gains_ref,
     keep_ref,
     weight,
@@ -62,7 +66,6 @@
     attended,
     mixed_out,
     mixed_in,
-    partial,
     load_sem,
     normed_sem,
     query_sem,
@@ -91,26 +94,53 @@
     units = 2 * heads
     patch = 2 * rows
 
-    loads = [
-        pltpu.make_async_copy(weight_hbm.at[c], weight.at[c], load_sem.at[c]) for c in range(3)
-    ]
-    loads.append(pltpu.make_async_copy(stale_hbm, stale, load_sem.at[3]))
-    loads.append(pltpu.make_async_copy(text_hbm, text, load_sem.at[4]))
-    loads.append(pltpu.make_async_copy(output_weight_hbm, output_weight, load_sem.at[5]))
+    factor = head ** (-0.5) * log2_e
+    pair = 2 if heads % 2 == 0 else 1
+    span = pair * head
+    pairs = heads // pair
+    early = min(3, heads)
+
+    def columns(step_index):
+        return pl.ds(pl.multiple_of(step_index * span, span), span)
+
+    def load(place, source, target):
+        return pltpu.make_async_copy(source, target, load_sem.at[place])
+
     small = [
-        pltpu.make_async_copy(source, target, load_sem.at[6 + place])
+        load(place, source, target)
         for place, (source, target) in enumerate(
             (
                 (tokens_hbm, tokens_ref),
                 (modulation_hbm, modulation_ref),
                 (gains_hbm, gains_ref),
-                (keep_hbm, keep_ref),
             )
         )
     ]
-    for load in small:
-        load.start()
-    loads[0].start()
+    query_weights = [
+        load(3 + c, weight_hbm.at[0, :, columns(c)], weight.at[0, :, columns(c)])
+        for c in range(pairs)
+    ]
+    place = 3 + pairs
+    key_weights = load(place, weight_hbm.at[1], weight.at[1])
+    value_weights = load(place + 1, weight_hbm.at[2], weight.at[2])
+    stale_load = load(place + 2, stale_hbm, stale)
+    text_load = load(place + 3, text_hbm, text)
+    keep_load = load(place + 4, keep_hbm, keep_ref)
+    order_load = load(place + 5, order_hbm, order_ref)
+    count_load = load(place + 6, count_hbm, count_ref)
+    turned = width - span
+    output_loads = [
+        load(place + 7, output_weight_hbm.at[turned:width], output_weight.at[0:span]),
+        load(place + 9, output_weight_hbm.at[turned - head : turned], last_weight),
+    ]
+    if turned > 0:
+        output_loads.append(
+            load(place + 8, output_weight_hbm.at[0:turned], output_weight.at[span:width])
+        )
+    for copy in small:
+        copy.start()
+    for c in range(pairs):
+        query_weights[pairs - 1 - c].start()
 
     barrier = pltpu.get_barrier_semaphore()
     pl.semaphore_signal(barrier, inc=1, device_id={"head": other_core}, device_id_type=MESH)
@@ -124,8 +154,8 @@
     def _():
         pl.semaphore_signal(barrier, inc=1, device_id={"section": behind}, device_id_type=MESH)
 
-    for load in small:
-        load.wait()
+    for copy in small:
+        copy.wait()
     hidden = tokens_ref[...].astype(f32)
     shifted = hidden - jnp.mean(hidden, axis=-1, keepdims=True)
     spread = jnp.mean(shifted * shifted, axis=-1, keepdims=True)
@@ -133,10 +163,6 @@
         shifted * lax.rsqrt(spread + epsilon) * (1.0 + modulation_ref[1:2, :])
         + modulation_ref[0:1, :]
     ).astype(bf16)
-
-    pl.semaphore_wait(
-        barrier, 2 + has_ahead.astype(jnp.int32) + has_behind.astype(jnp.int32)
-    )
 
     normed_copy = pltpu.make_async_remote_copy(
         src_ref=normed.at[0],
@@ -146,7 +172,6 @@
         device_id={"head": other_core},
         device_id_type=MESH,
     )
-    normed_copy.start()
 
     def remote(source, target, sems, unit, device):
         return pltpu.make_async_remote_copy(
@@ -176,25 +201,16 @@
             remote(back_total_out, back_total_in, back_total_sem, unit, mate),
         )
 
-    factor = head ** (-0.5) * log2_e
-    pair = 2 if heads % 2 == 0 else 1
-    span = pair * head
-
-    def columns(step_index):
-        return pl.ds(pl.multiple_of(step_index * span, span), span)
-
-    def project_queries(half):
-        @pl.loop(0, heads // pair)
-        def _(c):
-            part = jnp.dot(normed[half], weight[0, :, columns(c)], preferred_element_type=f32)
-            for j in range(pair):
-                unit = half * heads + c * pair + j
-                query[unit] = (
-                    head_norm(part[:, j * head : (j + 1) * head], gains_ref[0:1, :]) * factor
-                ).astype(bf16)
-                query_copy(unit).start()
-
-    early = min(3, heads)
+    def project_queries(half, c, first):
+        part = jnp.dot(normed[half], weight[0, :, columns(c)], preferred_element_type=f32)
+        for j in range(pair):
+            query[first + j] = (
+                head_norm(part[:, j * head : (j + 1) * head], gains_ref[0:1, :]) * factor
+            ).astype(bf16)
+
+    def send_queries(first):
+        for j in range(pair):
+            query_copy(first + j).start()
 
     def forward(unit):
         query_copy(unit).wait_recv()
@@ -203,14 +219,37 @@
         def _():
             forward_copy(unit, ahead).start()
 
-    for load in loads[1:]:
-        load.start()
-    loads[0].wait()
-    project_queries(0)
+    query_weights[pairs - 1].wait()
+    project_queries(0, pairs - 1, 0)
+
+    pl.semaphore_wait(
+        barrier, 2 + has_ahead.astype(jnp.int32) + has_behind.astype(jnp.int32)
+    )
+
+    normed_copy.start()
+    send_queries(0)
+    for copy in (key_weights, value_weights, stale_load, text_load, keep_load, order_load, count_load):
+        copy.start()
+    for copy in output_loads:
+        copy.start()
+    for c in range(pairs - 1):
+        query_weights[c].wait()
+
+    @pl.loop(0, pairs - 1)
+    def _(c):
+        project_queries(0, c, pair + heads + c * pair)
+
     normed_copy.wait_recv()
-    project_queries(1)
-    loads[1].wait()
-    loads[2].wait()
+
+    @pl.loop(0, pairs)
+    def _(c):
+        project_queries(1, c, pair + c * pair)
+        send_queries(pair + c * pair)
+
+    for c in range(pairs - 1):
+        send_queries(pair + heads + c * pair)
+    key_weights.wait()
+    value_weights.wait()
     own_rows = pl.ds(pl.multiple_of(core * rows, rows), rows)
     other_rows = pl.ds(pl.multiple_of(other_core * rows, rows), rows)
 
@@ -233,8 +272,8 @@
     def _(i):
         forward(i)
 
-    loads[3].wait()
-    loads[4].wait()
+    for copy in (stale_load, text_load, keep_load, order_load, count_load):
+        copy.wait()
 
     keep_row = keep_ref[pl.ds(pl.multiple_of(me * patch, patch), patch)].astype(f32)
     keep = jnp.transpose(jnp.broadcast_to(keep_row[None, :], (head, patch)))
@@ -287,8 +326,6 @@
         for copy in back_copies(unit):
             copy.start()
 
-    ahead_backs = min(2, heads)
-
     @pl.loop(early, units + 2 * early)
     def _(i):
         @pl.when(i < units)
@@ -299,7 +336,7 @@
 
         @pl.when(unit < units)
         def _():
-            h = lax.rem(unit, heads)
+            h = lax.rem(unit + heads - pair, heads)
 
             @pl.when(has_behind)
             def _():
@@ -317,32 +354,24 @@
                 query[unit], text_keys[h], text_values[h]
             )
 
-        @pl.when(jnp.logical_and(i >= units - ahead_backs, i < units))
-        def _():
-            send_back(i - units + ahead_backs)
-
-        @pl.when(i >= heads + 2 * early)
+        @pl.when(i >= 2 * early)
         def _():
             send_back(i - 2 * early)
 
-    @pl.loop(ahead_backs, heads)
-    def _(i):
-        send_back(i)
-
-    def gather_range(half, first, last):
-        @pl.loop(first, last)
-        def _(h):
-            unit = half * heads + h
-            for copy in back_copies(unit):
-                copy.wait_recv()
-            total = jnp.transpose(
-                jnp.broadcast_to(back_total_in[unit], (head, rows))
-            )
-            mine = own_sum[unit]
-            attended[half, :, pl.ds(pl.multiple_of(h * head, head), head)] = (
-                (mine[:, 0:head] + back_in[unit].astype(f32))
-                / (mine[:, head : 2 * head] + total)
-            ).astype(bf16)
+    def gathered(unit):
+        for copy in back_copies(unit):
+            copy.wait_recv()
+        total = jnp.transpose(jnp.broadcast_to(back_total_in[unit], (head, rows)))
+        mine = own_sum[unit]
+        return (
+            (mine[:, 0:head] + back_in[unit].astype(f32)) / (mine[:, head : 2 * head] + total)
+        ).astype(bf16)
+
+    def gather_range(half, first, last_unit, place):
+        @pl.loop(first, last_unit)
+        def _(unit):
+            lanes = pl.ds(pl.multiple_of((unit + place - first) * head, head), head)
+            attended[half, :, lanes] = gathered(unit)
 
     mixed_copy = pltpu.make_async_remote_copy(
         src_ref=mixed_out,
@@ -355,8 +384,10 @@
     full = output_weight.shape[1]
     wide = 512 if full % 512 == 0 else full
 
-    gather_range(1, 0, heads)
-    loads[5].wait()
+    for copy in output_loads:
+        copy.wait()
+    gather_range(1, pair, pair + heads - pair, pair)
+    gather_range(1, heads, pair + heads, 0)
 
     @pl.loop(0, full // wide)
     def _(c):
@@ -366,39 +397,20 @@
         ).astype(bf16)
 
     mixed_copy.start()
-    split = heads - min(2, heads - 1)
-    gather_range(0, 0, split)
+    gather_range(0, 0, pair, 0)
+    gather_range(0, pair + heads, units - 1, pair)
+    most = width - head
+    mixed_copy.wait_recv()
 
     @pl.loop(0, full // wide)
     def _(c):
         here = pl.ds(pl.multiple_of(c * wide, wide), wide)
-        partial[:, here] = jnp.dot(
-            attended[0, :, 0 : split * head],
-            output_weight[0 : split * head, here],
-            preferred_element_type=f32,
-        )
-
-    mixed_copy.wait_recv()
-
-    @pl.loop(0, full // wide)
-    def _(c):
-        here = pl.ds(pl.multiple_of(c * wide, wide), wide)
-        partial[:, here] = partial[:, here] + mixed_in[:, here].astype(f32)
-
-    gather_range(0, split, heads)
-
-    @pl.loop(0, full // wide)
-    def _(c):
-        here = pl.ds(pl.multiple_of(c * wide, wide), wide)
-        mixed = partial[:, here] + jnp.dot(
-            attended[0, :, split * head :],
-            output_weight[split * head :, here],
-            preferred_element_type=f32,
-        )
-        updated_ref[:, here] = (
-            tokens_ref[:, here].astype(f32) + modulation_ref[2:3, here] * mixed
-        ).astype(bf16)
-
+        mixed = mixed_in[:, here].astype(f32) + jnp.dot(
+            attended[0, :, 0:most], output_weight[0:most, here], preferred_element_type=f32
+        )
+        base[:, here] = tokens_ref[:, here].astype(f32) + modulation_ref[2:3, here] * mixed
+
+    last[...] = gathered(units - 1)
     normed_copy.wait_send()
     mixed_copy.wait_send()
 
@@ -416,6 +428,28 @@
         def _():
             for copy in far_copies(i, mate):
                 copy.wait_send()
+
+
+def finish(base, last, last_weight, modulation, raw, updated_hbm, raw_hbm, updated, sems):
+    full = base.shape[1]
+    wide = 512 if full % 512 == 0 else full
+    raw_copy = pltpu.make_async_copy(raw, raw_hbm, sems.at[0])
+    raw_copy.start()
+    copies = []
+    for c in range(full // wide):
+        here = slice(c * wide, (c + 1) * wide)
+        updated[:, here] = (
+            base[:, here]
+            + modulation[2:3, here]
+            * jnp.dot(last[...], last_weight[:, here], preferred_element_type=f32)
+        ).astype(bf16)
+        copies.append(
+            pltpu.make_async_copy(updated.at[:, here], updated_hbm.at[:, here], sems.at[1 + c])
+        )
+        copies[c].start()
+    for copy in copies:
+        copy.wait()
+    raw_copy.wait()
 
 
 def on_device(
@@ -437,24 +471,28 @@
     text_rows = text_cache.shape[1]
     heads = width // head
     units = 2 * heads
-    smem = pl.BlockSpec(memory_space=pltpu.SMEM)
+    pairs = heads // (2 if heads % 2 == 0 else 1)
     vmem = pl.BlockSpec(memory_space=pltpu.VMEM)
     hbm = pl.BlockSpec(memory_space=pl.ANY)
     unit_rows = pltpu.VMEM((units, rows, head), bf16)
     unit_totals = pltpu.VMEM((units, 1, rows), f32)
     unit_sums = pltpu.VMEM((units, rows, 2 * head), f32)
     unit_sems = pltpu.SemaphoreType.DMA((2, units))
-    return pl.pallas_call(
+    handed = pl.pallas_call(
         kernel,
         out_shape=(
-            pltpu.VMEM(video_tokens.shape, bf16),
+            pltpu.VMEM(video_tokens.shape, f32),
+            pltpu.VMEM((rows, head), bf16),
+            pltpu.VMEM((head, model), bf16),
+            pltpu.VMEM(modulation.shape, f32),
             pltpu.VMEM(stale_cache.shape, bf16),
         ),
-        in_specs=[smem, smem] + [hbm] * 8,
-        out_specs=(vmem, vmem),
+        in_specs=[hbm] * 10,
+        out_specs=(vmem,) * 5,
         scratch_shapes=[
+            pltpu.SMEM(patch_order.shape, jnp.int32),
+            pltpu.SMEM(text_count.shape, jnp.int32),
             pltpu.VMEM(video_tokens.shape, bf16),
-            pltpu.VMEM(modulation.shape, f32),
             pltpu.VMEM(norm_gains.shape, f32),
             pltpu.VMEM(video_keep.shape, jnp.int32),
             pltpu.VMEM(project_weight.shape, bf16),
@@ -482,8 +520,7 @@
             pltpu.VMEM((2, rows, width), bf16),
             pltpu.VMEM((rows, model), bf16),
             pltpu.VMEM((rows, model), bf16),
-            pltpu.VMEM((rows, model), f32),
-            pltpu.SemaphoreType.DMA((10,)),
+            pltpu.SemaphoreType.DMA((13 + pairs,)),
             pltpu.SemaphoreType.DMA((2,)),
             unit_sems,
             unit_sems,
@@ -494,7 +531,7 @@
             pltpu.SemaphoreType.DMA((2,)),
         ],
         compiler_params=pltpu.CompilerParams(
-            collective_id=0, has_side_effects=True, vmem_limit_bytes=60 * 1024 * 1024
+            collective_id=0, has_side_effects=True, vmem_limit_bytes=52 * 1024 * 1024
         ),
     )(
         patch_order,
@@ -508,6 +545,20 @@
         text_cache,
         stale_cache,
     )
+    return pl.pallas_call(
+        finish,
+        out_shape=(
+            jax.ShapeDtypeStruct(video_tokens.shape, bf16),
+            jax.ShapeDtypeStruct(stale_cache.shape, bf16),
+        ),
+        in_specs=[vmem] * 5,
+        out_specs=(hbm, hbm),
+        scratch_shapes=[
+            pltpu.VMEM(video_tokens.shape, bf16),
+            pltpu.SemaphoreType.DMA((1 + model // (512 if model % 512 == 0 else model),)),
+        ],
+        compiler_params=pltpu.CompilerParams(vmem_limit_bytes=16 * 1024 * 1024),
+    )(*[pltpu.with_memory_space_constraint(array, pltpu.VMEM) for array in handed])
 
 
 def solution(mesh):

time: 49.4 us -> 44.5 us (0.901)
  Pallas kernels: 46 us -> 43.1 us
  local copies, waits for them, and re-layouts: 2.02 us -> 0 us
    pallas_call x1 -> x2, Pallas kernels: 46 us -> 43.1 us  [the longest x1 41.6 us: on_device(): pl.pallas_call(kernel, out_shape=(pltpu.VMEM(video_tokens.shape, f32), pl...]
    unnamed x2 -> x0, local copies, waits for them, and re-layouts: 2.02 us -> none
where the time goes in v1:
time: 44.5 us; the launch traced here: 44.3 us
  Pallas kernels  43.1 us (97%)
  between operations  1.29 us (3%)
    pallas_call x1, Pallas kernels, on_device(): pl.pallas_call(kernel, out_shape=(pltpu.VMEM(video_tokens.shape, f32), pl...  41.6 us
    pallas_call x1, Pallas kernels, on_device(): pl.pallas_call(finish, out_shape=(jax.ShapeDtypeStruct(video_tokens.shape...  1.44 us

profile of v1, /device:TPU:0, one launch (start us, length us, event | category | flops | bytes accessed | tf_op | source)
XLA Modules:
  0.0 44.3 jit_solution(18092294667495495312)
XLA Ops:
  1.3 41.6 %shard_map.113 = (f32[256,1536]{1,0:T(8,128)S(1)}, bf16[256,128]{1,0:T(8,128)(2,1)S(1)}, bf16[128,1536]{1,0:T(8,128)(2,1)S(1)}, f32[3,1536]{1,0:T(4,128)S(1)}, bf16[2,512,768]{2,1,0:T(8,128)(2,1)S(1)}) custom-call(s32[8]{0:T(128)} %order_hbm.1, s32[1]{0:T(128)S(6)} %copy.12.count_hbm, bf16[256,1536]{1,0:T(8,128)(2,1)} %tokens_hbm.1, ...), custom_call_target="tpu_custom_call" | custom-call | tf_op jit(solution)/shard_map/pallas_call | solution.py:481
  42.9 1.4 %shard_map.114 = (bf16[256,1536]{1,0:T(8,128)(2,1)}, bf16[2,512,768]{2,1,0:T(8,128)(2,1)}) custom-call(f32[256,1536]{1,0:T(8,128)S(1)} %get-tuple-element.7.base, bf16[256,128]{1,0:T(8,128)(2,1)S(1)} %get-tuple-element.8.last, bf16[128,1536]{1,0:T(8,128)(2,1)S(1)} %get-tuple-element.9.last_weight, f32[3,1536]{1,0:T(4,128)S(1)} %get-tuple-element.10.modulation, ...), custom_call_target="tpu_custom_call" | custom-call | tf_op jit(solution)/shard_map/pallas_call | solution.py:548

commit v2 on v1

--- a/solution.py
+++ b/solution.py
@@ -67,6 +67,7 @@
     mixed_out,
     mixed_in,
     load_sem,
+    send_sem,
     normed_sem,
     query_sem,
     forward_sem,
@@ -75,6 +76,7 @@
     back_sem,
     back_total_sem,
     mixed_sem,
+    present_sem,
 ):
     count = lax.axis_size("section")
     me = lax.axis_index("section")
@@ -87,6 +89,19 @@
     behind = me - step
     has_ahead = jnp.logical_and(ahead >= 0, ahead < count)
     has_behind = jnp.logical_and(behind >= 0, behind < count)
+    barrier = pltpu.get_barrier_semaphore()
+    pl.semaphore_signal(barrier, inc=1, device_id={"head": other_core}, device_id_type=MESH)
+    pl.semaphore_signal(barrier, inc=1, device_id={"section": mate}, device_id_type=MESH)
+
+    later = me + 2
+    earlier = me - 2
+    has_later = later < count
+    has_earlier = earlier >= 0
+
+    @pl.when(has_later)
+    def _():
+        pl.semaphore_signal(barrier, inc=1, device_id={"section": later}, device_id_type=MESH)
+
     rows = tokens_hbm.shape[0]
     head = gains_ref.shape[1]
     width = weight.shape[2]
@@ -98,7 +113,10 @@
     pair = 2 if heads % 2 == 0 else 1
     span = pair * head
     pairs = heads // pair
-    early = min(3, heads)
+    lag = pair + 1
+    back_lag = 3 * pair
+    ready = 1
+    groups = 2 * pairs
 
     def columns(step_index):
         return pl.ds(pl.multiple_of(step_index * span, span), span)
@@ -110,96 +128,120 @@
         load(place, source, target)
         for place, (source, target) in enumerate(
             (
-                (tokens_hbm, tokens_ref),
                 (modulation_hbm, modulation_ref),
                 (gains_hbm, gains_ref),
             )
         )
     ]
-    query_weights = [
-        load(3 + c, weight_hbm.at[0, :, columns(c)], weight.at[0, :, columns(c)])
-        for c in range(pairs)
+    half_rows = rows // 2
+    slabs = [slice(0, half_rows), slice(half_rows, rows)]
+    token_loads = [
+        load(2 + place, tokens_hbm.at[slab], tokens_ref.at[slab])
+        for place, slab in enumerate(slabs)
     ]
-    place = 3 + pairs
-    key_weights = load(place, weight_hbm.at[1], weight.at[1])
-    value_weights = load(place + 1, weight_hbm.at[2], weight.at[2])
-    stale_load = load(place + 2, stale_hbm, stale)
-    text_load = load(place + 3, text_hbm, text)
-    keep_load = load(place + 4, keep_hbm, keep_ref)
-    order_load = load(place + 5, order_hbm, order_ref)
-    count_load = load(place + 6, count_hbm, count_ref)
-    turned = width - span
+    rest = width - span
+    first_weights = load(4, weight_hbm.at[0, :, rest:width], weight.at[0, :, rest:width])
+    other_weights = load(5, weight_hbm.at[0, :, 0:rest], weight.at[0, :, 0:rest])
+    cache_weights = load(6, weight_hbm.at[1:3], weight.at[1:3])
+    stale_load = load(7, stale_hbm, stale)
+    text_load = load(8, text_hbm, text)
+    keep_load = load(9, keep_hbm, keep_ref)
+    order_load = load(10, order_hbm, order_ref)
+    count_load = load(11, count_hbm, count_ref)
+    last_row = max(rest - span, 0)
     output_loads = [
-        load(place + 7, output_weight_hbm.at[turned:width], output_weight.at[0:span]),
-        load(place + 9, output_weight_hbm.at[turned - head : turned], last_weight),
+        load(12, output_weight_hbm.at[rest:width], output_weight.at[0:span]),
+        load(13, output_weight_hbm.at[last_row : last_row + span], last_weight),
     ]
-    if turned > 0:
+    if rest > 0:
         output_loads.append(
-            load(place + 8, output_weight_hbm.at[0:turned], output_weight.at[span:width])
-        )
+            load(14, output_weight_hbm.at[0:rest], output_weight.at[span:width])
+        )
+    token_loads[0].start()
     for copy in small:
         copy.start()
-    for c in range(pairs):
-        query_weights[pairs - 1 - c].start()
-
-    barrier = pltpu.get_barrier_semaphore()
-    pl.semaphore_signal(barrier, inc=1, device_id={"head": other_core}, device_id_type=MESH)
-    pl.semaphore_signal(barrier, inc=1, device_id={"section": mate}, device_id_type=MESH)
-
-    @pl.when(has_ahead)
-    def _():
-        pl.semaphore_signal(barrier, inc=1, device_id={"section": ahead}, device_id_type=MESH)
-
-    @pl.when(has_behind)
-    def _():
-        pl.semaphore_signal(barrier, inc=1, device_id={"section": behind}, device_id_type=MESH)
-
-    for copy in small:
-        copy.wait()
-    hidden = tokens_ref[...].astype(f32)
-    shifted = hidden - jnp.mean(hidden, axis=-1, keepdims=True)
-    spread = jnp.mean(shifted * shifted, axis=-1, keepdims=True)
-    normed[0] = (
-        shifted * lax.rsqrt(spread + epsilon) * (1.0 + modulation_ref[1:2, :])
-        + modulation_ref[0:1, :]
-    ).astype(bf16)
-
-    normed_copy = pltpu.make_async_remote_copy(
-        src_ref=normed.at[0],
-        dst_ref=normed.at[1],
-        send_sem=normed_sem.at[0],
-        recv_sem=normed_sem.at[1],
-        device_id={"head": other_core},
-        device_id_type=MESH,
-    )
-
-    def remote(source, target, sems, unit, device):
+    first_weights.start()
+    token_loads[1].start()
+    if rest > 0:
+        other_weights.start()
+
+    def normalize(slab):
+        hidden = tokens_ref[slab].astype(f32)
+        shifted = hidden - jnp.mean(hidden, axis=-1, keepdims=True)
+        spread = jnp.mean(shifted * shifted, axis=-1, keepdims=True)
+        normed[0, slab] = (
+            shifted * lax.rsqrt(spread + epsilon) * (1.0 + modulation_ref[1:2, :])
+            + modulation_ref[0:1, :]
+        ).astype(bf16)
+
+    normed_copies = [
+        pltpu.make_async_remote_copy(
+            src_ref=normed.at[0, slab],
+            dst_ref=normed.at[1, slab],
+            send_sem=send_sem.at[0],
+            recv_sem=normed_sem.at[place],
+            device_id={"head": other_core},
+            device_id_type=MESH,
+        )
+        for place, slab in enumerate(slabs)
+    ]
+
+    def remote(source, target, kind, sem, first, number, device):
         return pltpu.make_async_remote_copy(
-            src_ref=source.at[unit],
-            dst_ref=target.at[unit],
-            send_sem=sems.at[0, unit],
-            recv_sem=sems.at[1, unit],
+            src_ref=source.at[pl.ds(first, number)],
+            dst_ref=target.at[pl.ds(first, number)],
+            send_sem=send_sem.at[kind],
+            recv_sem=sem,
             device_id={"section": device},
             device_id_type=MESH,
         )
 
-    def query_copy(unit):
-        return remote(query, query_mate, query_sem, unit, mate)
+    def query_copy(group):
+        return remote(query, query_mate, 1, query_sem.at[group + 1], group * pair, pair, mate)
+
+    def first_copy(place):
+        return pltpu.make_async_remote_copy(
+            src_ref=query.at[0:pair, slabs[place]],
+            dst_ref=query_mate.at[0:pair, slabs[place]],
+            send_sem=send_sem.at[1],
+            recv_sem=query_sem.at[place],
+            device_id={"section": mate},
+            device_id_type=MESH,
+        )
 
     def forward_copy(unit, device):
-        return remote(query_mate, query_far, forward_sem, unit, device)
-
-    def far_copies(unit, device):
-        return (
-            remote(far_out, far_in, far_sem, unit, device),
-            remote(far_total_out, far_total_in, far_total_sem, unit, device),
-        )
-
-    def back_copies(unit):
-        return (
-            remote(back_out, back_in, back_sem, unit, mate),
-            remote(back_total_out, back_total_in, back_total_sem, unit, mate),
-        )
+        return remote(query_mate, query_far, 2, forward_sem.at[unit], unit, 1, device)
+
+    def far_copy(unit, device):
+        return remote(far_out, far_in, 3, far_sem.at[unit], unit, 1, device)
+
+    def far_total_copy(group, device):
+        return remote(
+            far_total_out, far_total_in, 4, far_total_sem.at[group], group * pair, pair, device
+        )
+
+    def back_copy(group):
+        return remote(back_out, back_in, 5, back_sem.at[group], group * pair, pair, mate)
+
+    total_parts = [(0, pair + heads)]
+    for first in range(pair + heads, units, pair):
+        total_parts.append((first, pair))
+
+    def back_total_copy(part):
+        first, number = total_parts[part]
+        return remote(
+            back_total_out, back_total_in, 6, back_total_sem.at[part], first, number, mate
+        )
+
+    def sent(source, target, kind, axis, device):
+        return pltpu.make_async_remote_copy(
+            src_ref=source,
+            dst_ref=target,
+            send_sem=send_sem.at[kind],
+            recv_sem=mixed_sem.at[0],
+            device_id={axis: device},
+            device_id_type=MESH,
+        ).wait_send()
 
     def project_queries(half, c, first):
         part = jnp.dot(normed[half], weight[0, :, columns(c)], preferred_element_type=f32)
@@ -208,48 +250,82 @@
                 head_norm(part[:, j * head : (j + 1) * head], gains_ref[0:1, :]) * factor
             ).astype(bf16)
 
-    def send_queries(first):
+    def forward(group):
+        @pl.when(group == 0)
+        def _():
+            for place in range(2):
+                first_copy(place).wait_recv()
+
+        @pl.when(group > 0)
+        def _():
+            query_copy(group).wait_recv()
+
+        @pl.when(has_ahead)
+        def _():
+            for j in range(pair):
+                forward_copy(group * pair + j, ahead).start()
+
+    def first_queries(place):
+        slab = slabs[place]
+        part = jnp.dot(
+            normed[0, slab], weight[0, :, width - span : width], preferred_element_type=f32
+        )
         for j in range(pair):
-            query_copy(first + j).start()
-
-    def forward(unit):
-        query_copy(unit).wait_recv()
-
-        @pl.when(has_ahead)
-        def _():
-            forward_copy(unit, ahead).start()
-
-    query_weights[pairs - 1].wait()
-    project_queries(0, pairs - 1, 0)
-
-    pl.semaphore_wait(
-        barrier, 2 + has_ahead.astype(jnp.int32) + has_behind.astype(jnp.int32)
-    )
-
-    normed_copy.start()
-    send_queries(0)
-    for copy in (key_weights, value_weights, stale_load, text_load, keep_load, order_load, count_load):
+            query[j, slab] = (
+                head_norm(part[:, j * head : (j + 1) * head], gains_ref[0:1, :]) * factor
+            ).astype(bf16)
+
+    def send_first(place):
+        normed_copies[place].start()
+        first_copy(place).start()
+
+    token_loads[0].wait()
+    for copy in small:
+        copy.wait()
+    normalize(slabs[0])
+    first_weights.wait()
+    first_queries(0)
+
+    pl.semaphore_wait(barrier, 2 + has_earlier.astype(jnp.int32))
+
+    @pl.when(has_earlier)
+    def _():
+        pl.semaphore_signal(
+            present_sem, inc=1, device_id={"section": earlier}, device_id_type=MESH
+        )
+
+    send_first(0)
+    token_loads[1].wait()
+    normalize(slabs[1])
+    first_queries(1)
+    send_first(1)
+    for copy in (cache_weights, stale_load, text_load, keep_load, order_load, count_load):
         copy.start()
     for copy in output_loads:
         copy.start()
-    for c in range(pairs - 1):
-        query_weights[c].wait()
+    if rest > 0:
+        other_weights.wait()
 
     @pl.loop(0, pairs - 1)
     def _(c):
         project_queries(0, c, pair + heads + c * pair)
 
-    normed_copy.wait_recv()
+    for copy in normed_copies:
+        copy.wait_recv()
 
     @pl.loop(0, pairs)
     def _(c):
         project_queries(1, c, pair + c * pair)
-        send_queries(pair + c * pair)
+        query_copy(1 + c).start()
 
     for c in range(pairs - 1):
-        send_queries(pair + heads + c * pair)
-    key_weights.wait()
-    value_weights.wait()
+        query_copy(1 + pairs + c).start()
+
+    @pl.when(has_later)
+    def _():
+        pl.semaphore_wait(present_sem, 1)
+
+    cache_weights.wait()
     own_rows = pl.ds(pl.multiple_of(core * rows, rows), rows)
     other_rows = pl.ds(pl.multiple_of(other_core * rows, rows), rows)
 
@@ -264,13 +340,10 @@
             raw[w, own_rows, columns(c)] = part[0:rows]
             raw[w, other_rows, columns(c)] = part[rows:patch]
 
-        @pl.when(c < early)
-        def _():
-            forward(c)
-
-    @pl.loop(min(early, heads // pair), early)
-    def _(i):
-        forward(i)
+        @pl.when(c == min(1, pairs - 1))
+        def _():
+            forward(0)
+
 
     for copy in (stale_load, text_load, keep_load, order_load, count_load):
         copy.wait()
@@ -309,58 +382,83 @@
 
     def send_back(unit):
         numerator = mate_sum[unit, :, 0:head]
-        totals = total_rows(mate_sum[unit])
+        last_of_pair = lax.rem(unit, pair) == pair - 1
+        group = unit // pair
 
         @pl.when(has_ahead)
         def _():
-            for copy in far_copies(unit, mate):
-                copy.wait_recv()
+            far_copy(unit, mate).wait_recv()
             back_out[unit] = (numerator + far_in[unit].astype(f32)).astype(bf16)
-            back_total_out[unit] = totals + far_total_in[unit]
 
         @pl.when(jnp.logical_not(has_ahead))
         def _():
             back_out[unit] = numerator.astype(bf16)
-            back_total_out[unit] = totals
-
-        for copy in back_copies(unit):
-            copy.start()
-
-    @pl.loop(early, units + 2 * early)
+
+        @pl.when(last_of_pair)
+        def _():
+            mine = [group * pair + j for j in range(pair)]
+
+            @pl.when(has_ahead)
+            def _():
+                far_total_copy(group, mate).wait_recv()
+                for one in mine:
+                    back_total_out[one] = total_rows(mate_sum[one]) + far_total_in[one]
+
+            @pl.when(jnp.logical_not(has_ahead))
+            def _():
+                for one in mine:
+                    back_total_out[one] = total_rows(mate_sum[one])
+
+            for part, (first, number) in enumerate(total_parts):
+
+                @pl.when(unit == first + number - 1)
+                def _():
+                    back_total_copy(part).start()
+
+            back_copy(group).start()
+
+    @pl.loop(ready * pair, units + back_lag)
     def _(i):
-        @pl.when(i < units)
-        def _():
-            forward(i)
-
-        unit = i - early
-
-        @pl.when(unit < units)
+        @pl.when(jnp.logical_and(i < units, lax.rem(i, pair) == 0))
+        def _():
+            forward(i // pair)
+
+        unit = i - lag
+
+        @pl.when(jnp.logical_and(unit >= 0, unit < units))
         def _():
             h = lax.rem(unit + heads - pair, heads)
 
             @pl.when(has_behind)
             def _():
                 forward_copy(unit, mate).wait_recv()
-                summed = weighted(query_far[unit], keys[far_version, h], values[far_version, h])
-                far_out[unit] = summed[:, 0:head].astype(bf16)
-                far_total_out[unit] = total_rows(summed)
-                for copy in far_copies(unit, behind):
-                    copy.start()
-
+
+            far = weighted(query_far[unit], keys[far_version, h], values[far_version, h])
             mate_sum[unit] = weighted(
                 query_mate[unit], keys[mate_version, h], values[mate_version, h]
             )
             own_sum[unit] = weighted(query[unit], keys[0, h], values[0, h]) + weighted(
                 query[unit], text_keys[h], text_values[h]
             )
-
-        @pl.when(i >= 2 * early)
-        def _():
-            send_back(i - 2 * early)
+            far_out[unit] = far[:, 0:head].astype(bf16)
+            far_total_out[unit] = total_rows(far)
+
+            @pl.when(has_behind)
+            def _():
+                far_copy(unit, behind).start()
+
+                @pl.when(lax.rem(unit, pair) == pair - 1)
+                def _():
+                    far_total_copy(unit // pair, behind).start()
+
+        @pl.when(i >= back_lag)
+        def _():
+            send_back(i - back_lag)
+
+    def arrive(unit):
+        back_copy(unit // pair).wait_recv()
 
     def gathered(unit):
-        for copy in back_copies(unit):
-            copy.wait_recv()
         total = jnp.transpose(jnp.broadcast_to(back_total_in[unit], (head, rows)))
         mine = own_sum[unit]
         return (
@@ -368,16 +466,18 @@
         ).astype(bf16)
 
     def gather_range(half, first, last_unit, place):
-        @pl.loop(first, last_unit)
-        def _(unit):
-            lanes = pl.ds(pl.multiple_of((unit + place - first) * head, head), head)
-            attended[half, :, lanes] = gathered(unit)
+        @pl.loop(0, (last_unit - first) // pair)
+        def _(c):
+            arrive(first + c * pair)
+            for j in range(pair):
+                lanes = pl.ds(pl.multiple_of((place + c * pair + j) * head, head), head)
+                attended[half, :, lanes] = gathered(first + c * pair + j)
 
     mixed_copy = pltpu.make_async_remote_copy(
         src_ref=mixed_out,
         dst_ref=mixed_in,
-        send_sem=mixed_sem.at[0],
-        recv_sem=mixed_sem.at[1],
+        send_sem=send_sem.at[7],
+        recv_sem=mixed_sem.at[0],
         device_id={"head": other_core},
         device_id_type=MESH,
     )
@@ -386,6 +486,7 @@
 
     for copy in output_loads:
         copy.wait()
+    back_total_copy(0).wait_recv()
     gather_range(1, pair, pair + heads - pair, pair)
     gather_range(1, heads, pair + heads, 0)
 
@@ -398,8 +499,11 @@
 
     mixed_copy.start()
     gather_range(0, 0, pair, 0)
-    gather_range(0, pair + heads, units - 1, pair)
-    most = width - head
+    for part in range(1, len(total_parts) - 1):
+        first, number = total_parts[part]
+        back_total_copy(part).wait_recv()
+        gather_range(0, first, first + number, first - heads)
+    most = width - span
     mixed_copy.wait_recv()
 
     @pl.loop(0, full // wide)
@@ -410,24 +514,25 @@
         )
         base[:, here] = tokens_ref[:, here].astype(f32) + modulation_ref[2:3, here] * mixed
 
-    last[...] = gathered(units - 1)
-    normed_copy.wait_send()
+    if len(total_parts) > 1:
+        back_total_copy(len(total_parts) - 1).wait_recv()
+    arrive(units - pair)
+    for j in range(pair):
+        last[:, j * head : (j + 1) * head] = gathered(units - pair + j)
+    sent(normed.at[0], normed.at[1], 0, "head", other_core)
     mixed_copy.wait_send()
-
-    @pl.loop(0, units)
-    def _(i):
-        query_copy(i).wait_send()
-        for copy in back_copies(i):
-            copy.wait_send()
-
-        @pl.when(has_ahead)
-        def _():
-            forward_copy(i, mate).wait_send()
-
-        @pl.when(has_behind)
-        def _():
-            for copy in far_copies(i, mate):
-                copy.wait_send()
+    sent(query, query_mate, 1, "section", mate)
+    sent(back_out, back_in, 5, "section", mate)
+    sent(back_total_out, back_total_in, 6, "section", mate)
+
+    @pl.when(has_ahead)
+    def _():
+        sent(query_mate, query_far, 2, "section", mate)
+
+    @pl.when(has_behind)
+    def _():
+        sent(far_out, far_in, 3, "section", mate)
+        sent(far_total_out, far_total_in, 4, "section", mate)
 
 
 def finish(base, last, last_weight, modulation, raw, updated_hbm, raw_hbm, updated, sems):
@@ -471,19 +576,19 @@
     text_rows = text_cache.shape[1]
     heads = width // head
     units = 2 * heads
-    pairs = heads // (2 if heads % 2 == 0 else 1)
+    pair = 2 if heads % 2 == 0 else 1
+    pairs = heads // pair
     vmem = pl.BlockSpec(memory_space=pltpu.VMEM)
     hbm = pl.BlockSpec(memory_space=pl.ANY)
     unit_rows = pltpu.VMEM((units, rows, head), bf16)
     unit_totals = pltpu.VMEM((units, 1, rows), f32)
     unit_sums = pltpu.VMEM((units, rows, 2 * head), f32)
-    unit_sems = pltpu.SemaphoreType.DMA((2, units))
     handed = pl.pallas_call(
         kernel,
         out_shape=(
             pltpu.VMEM(video_tokens.shape, f32),
-            pltpu.VMEM((rows, head), bf16),
-            pltpu.VMEM((head, model), bf16),
+            pltpu.VMEM((rows, pair * head), bf16),
+            pltpu.VMEM((pair * head, model), bf16),
             pltpu.VMEM(modulation.shape, f32),
             pltpu.VMEM(stale_cache.shape, bf16),
         ),
@@ -520,15 +625,17 @@
             pltpu.VMEM((2, rows, width), bf16),
             pltpu.VMEM((rows, model), bf16),
             pltpu.VMEM((rows, model), bf16),
-            pltpu.SemaphoreType.DMA((13 + pairs,)),
+            pltpu.SemaphoreType.DMA((15,)),
+            pltpu.SemaphoreType.DMA((8,)),
             pltpu.SemaphoreType.DMA((2,)),
-            unit_sems,
-            unit_sems,
-            unit_sems,
-            unit_sems,
-            unit_sems,
-            unit_sems,
-            pltpu.SemaphoreType.DMA((2,)),
+            pltpu.SemaphoreType.DMA((2 * pairs + 1,)),
+            pltpu.SemaphoreType.DMA((units,)),
+            pltpu.SemaphoreType.DMA((units,)),
+            pltpu.SemaphoreType.DMA((2 * pairs,)),
+            pltpu.SemaphoreType.DMA((2 * pairs,)),
+            pltpu.SemaphoreType.DMA((pairs,)),
+            pltpu.SemaphoreType.DMA((1,)),
+            pltpu.SemaphoreType.REGULAR,
         ],
         compiler_params=pltpu.CompilerParams(
             collective_id=0, has_side_effects=True, vmem_limit_bytes=52 * 1024 * 1024

time: 44.5 us -> 43.5 us (0.978)
  Pallas kernels: 43.1 us -> 42.1 us
    pallas_call x1, Pallas kernels: 41.6 us -> 40.6 us  [on_device(): pl.pallas_call(kernel, out_shape=(pltpu.VMEM(video_tokens.shape, f32), pl...]
where the time goes in v2:
time: 43.5 us; the launch traced here: 43.4 us
  Pallas kernels  42.1 us (97%)
  between operations  1.29 us (3%)
    pallas_call x1, Pallas kernels, on_device(): pl.pallas_call(kernel, out_shape=(pltpu.VMEM(video_tokens.shape, f32), pl...  40.6 us
    pallas_call x1, Pallas kernels, on_device(): pl.pallas_call(finish, out_shape=(jax.ShapeDtypeStruct(video_tokens.shape...  1.45 us

profile of v2, /device:TPU:0, one launch (start us, length us, event | category | flops | bytes accessed | tf_op | source)
XLA Modules:
  0.0 43.4 jit_solution(4195000174012892377)
XLA Ops:
  1.3 40.6 %shard_map.113 = (f32[256,1536]{1,0:T(8,128)S(1)}, bf16[256,256]{1,0:T(8,128)(2,1)S(1)}, bf16[256,1536]{1,0:T(8,128)(2,1)S(1)}, f32[3,1536]{1,0:T(4,128)S(1)}, bf16[2,512,768]{2,1,0:T(8,128)(2,1)S(1)}) custom-call(s32[8]{0:T(128)} %order_hbm.1, s32[1]{0:T(128)S(6)} %copy.12.count_hbm, bf16[256,1536]{1,0:T(8,128)(2,1)} %tokens_hbm.1, ...), custom_call_target="tpu_custom_call" | custom-call | tf_op jit(solution)/shard_map/pallas_call | solution.py:586
  41.9 1.4 %shard_map.114 = (bf16[256,1536]{1,0:T(8,128)(2,1)}, bf16[2,512,768]{2,1,0:T(8,128)(2,1)}) custom-call(f32[256,1536]{1,0:T(8,128)S(1)} %get-tuple-element.7.base, bf16[256,256]{1,0:T(8,128)(2,1)S(1)} %get-tuple-element.8.last, bf16[256,1536]{1,0:T(8,128)(2,1)S(1)} %get-tuple-element.9.last_weight, f32[3,1536]{1,0:T(4,128)S(1)} %get-tuple-element.10.modulation, ...), custom_call_target="tpu_custom_call" | custom-call | tf_op jit(solution)/shard_map/pallas_call | solution.py:655

commit v3 on v2

--- a/solution.py
+++ b/solution.py
@@ -89,19 +89,6 @@
     behind = me - step
     has_ahead = jnp.logical_and(ahead >= 0, ahead < count)
     has_behind = jnp.logical_and(behind >= 0, behind < count)
-    barrier = pltpu.get_barrier_semaphore()
-    pl.semaphore_signal(barrier, inc=1, device_id={"head": other_core}, device_id_type=MESH)
-    pl.semaphore_signal(barrier, inc=1, device_id={"section": mate}, device_id_type=MESH)
-
-    later = me + 2
-    earlier = me - 2
-    has_later = later < count
-    has_earlier = earlier >= 0
-
-    @pl.when(has_later)
-    def _():
-        pl.semaphore_signal(barrier, inc=1, device_id={"section": later}, device_id_type=MESH)
-
     rows = tokens_hbm.shape[0]
     head = gains_ref.shape[1]
     width = weight.shape[2]
@@ -115,6 +102,7 @@
     pairs = heads // pair
     lag = pair + 1
     back_lag = 3 * pair
+    own_lag = 3 * pair
     ready = 1
     groups = 2 * pairs
 
@@ -158,6 +146,20 @@
             load(14, output_weight_hbm.at[0:rest], output_weight.at[span:width])
         )
     token_loads[0].start()
+
+    barrier = pltpu.get_barrier_semaphore()
+    pl.semaphore_signal(barrier, inc=1, device_id={"head": other_core}, device_id_type=MESH)
+    pl.semaphore_signal(barrier, inc=1, device_id={"section": mate}, device_id_type=MESH)
+
+    later = me + 2
+    earlier = me - 2
+    has_later = later < count
+    has_earlier = earlier >= 0
+
+    @pl.when(has_later)
+    def _():
+        pl.semaphore_signal(barrier, inc=1, device_id={"section": later}, device_id_type=MESH)
+
     for copy in small:
         copy.start()
     first_weights.start()
@@ -275,10 +277,6 @@
                 head_norm(part[:, j * head : (j + 1) * head], gains_ref[0:1, :]) * factor
             ).astype(bf16)
 
-    def send_first(place):
-        normed_copies[place].start()
-        first_copy(place).start()
-
     token_loads[0].wait()
     for copy in small:
         copy.wait()
@@ -294,11 +292,13 @@
             present_sem, inc=1, device_id={"section": earlier}, device_id_type=MESH
         )
 
-    send_first(0)
+    normed_copies[0].start()
+    first_copy(0).start()
     token_loads[1].wait()
     normalize(slabs[1])
+    normed_copies[1].start()
     first_queries(1)
-    send_first(1)
+    first_copy(1).start()
     for copy in (cache_weights, stale_load, text_load, keep_load, order_load, count_load):
         copy.start()
     for copy in output_loads:
@@ -377,6 +377,9 @@
         weights = jnp.exp2(dot_nt(queries, key_rows)).astype(bf16)
         return jnp.dot(weights, value_rows, preferred_element_type=f32)
 
+    def head_of(unit):
+        return lax.rem(unit + heads - pair, heads)
+
     def total_rows(summed):
         return jnp.transpose(summed[:, head : 2 * head])[0:1, :]
 
@@ -417,7 +420,7 @@
 
             back_copy(group).start()
 
-    @pl.loop(ready * pair, units + back_lag)
+    @pl.loop(ready * pair, units + max(back_lag, own_lag))
     def _(i):
         @pl.when(jnp.logical_and(i < units, lax.rem(i, pair) == 0))
         def _():
@@ -427,7 +430,7 @@
 
         @pl.when(jnp.logical_and(unit >= 0, unit < units))
         def _():
-            h = lax.rem(unit + heads - pair, heads)
+            h = head_of(unit)
 
             @pl.when(has_behind)
             def _():
@@ -437,9 +440,6 @@
             mate_sum[unit] = weighted(
                 query_mate[unit], keys[mate_version, h], values[mate_version, h]
             )
-            own_sum[unit] = weighted(query[unit], keys[0, h], values[0, h]) + weighted(
-                query[unit], text_keys[h], text_values[h]
-            )
             far_out[unit] = far[:, 0:head].astype(bf16)
             far_total_out[unit] = total_rows(far)
 
@@ -451,9 +451,18 @@
                 def _():
                     far_total_copy(unit // pair, behind).start()
 
-        @pl.when(i >= back_lag)
+        @pl.when(jnp.logical_and(i >= back_lag, i < units + back_lag))
         def _():
             send_back(i - back_lag)
+
+        own = i - own_lag
+
+        @pl.when(own >= 0)
+        def _():
+            h = head_of(own)
+            own_sum[own] = weighted(query[own], keys[0, h], values[0, h]) + weighted(
+                query[own], text_keys[h], text_values[h]
+            )
 
     def arrive(unit):
         back_copy(unit // pair).wait_recv()

time: 43.5 us -> 43.2 us (level)
  no operation moved by 1% of the time
where the time goes in v3:
time: 43.2 us; the launch traced here: 43.1 us
  Pallas kernels  41.8 us (97%)
  between operations  1.29 us (3%)
    pallas_call x1, Pallas kernels, on_device(): pl.pallas_call(kernel, out_shape=(pltpu.VMEM(video_tokens.shape, f32), pl...  40.3 us
    pallas_call x1, Pallas kernels, on_device(): pl.pallas_call(finish, out_shape=(jax.ShapeDtypeStruct(video_tokens.shape...  1.45 us

profile of v3, /device:TPU:0, one launch (start us, length us, event | category | flops | bytes accessed | tf_op | source)
XLA Modules:
  0.0 43.1 jit_solution(16125026502080126552)
XLA Ops:
  1.3 40.3 %shard_map.113 = (f32[256,1536]{1,0:T(8,128)S(1)}, bf16[256,256]{1,0:T(8,128)(2,1)S(1)}, bf16[256,1536]{1,0:T(8,128)(2,1)S(1)}, f32[3,1536]{1,0:T(4,128)S(1)}, bf16[2,512,768]{2,1,0:T(8,128)(2,1)S(1)}) custom-call(s32[8]{0:T(128)} %order_hbm.1, s32[1]{0:T(128)S(6)} %copy.12.count_hbm, bf16[256,1536]{1,0:T(8,128)(2,1)} %tokens_hbm.1, ...), custom_call_target="tpu_custom_call" | custom-call | tf_op jit(solution)/shard_map/pallas_call | solution.py:595
  41.6 1.4 %shard_map.114 = (bf16[256,1536]{1,0:T(8,128)(2,1)}, bf16[2,512,768]{2,1,0:T(8,128)(2,1)}) custom-call(f32[256,1536]{1,0:T(8,128)S(1)} %get-tuple-element.7.base, bf16[256,256]{1,0:T(8,128)(2,1)S(1)} %get-tuple-element.8.last, bf16[256,1536]{1,0:T(8,128)(2,1)S(1)} %get-tuple-element.9.last_weight, f32[3,1536]{1,0:T(4,128)S(1)} %get-tuple-element.10.modulation, ...), custom_call_target="tpu_custom_call" | custom-call | tf_op jit(solution)/shard_map/pallas_call | solution.py:664

commit v4 on v3

--- a/solution.py
+++ b/solution.py
@@ -22,7 +22,7 @@
 
 def kernel(
     order_hbm,
-    count_hbm,
+    count_ref,
     tokens_hbm,
     modulation_hbm,
     gains_hbm,
@@ -37,7 +37,6 @@
     modulation_ref,
     raw,
     order_ref,
-    count_ref,
     tokens_ref,
     gains_ref,
     keep_ref,
@@ -104,7 +103,6 @@
     back_lag = 3 * pair
     own_lag = 3 * pair
     ready = 1
-    groups = 2 * pairs
 
     def columns(step_index):
         return pl.ds(pl.multiple_of(step_index * span, span), span)
@@ -135,15 +133,14 @@
     text_load = load(8, text_hbm, text)
     keep_load = load(9, keep_hbm, keep_ref)
     order_load = load(10, order_hbm, order_ref)
-    count_load = load(11, count_hbm, count_ref)
     last_row = max(rest - span, 0)
     output_loads = [
-        load(12, output_weight_hbm.at[rest:width], output_weight.at[0:span]),
-        load(13, output_weight_hbm.at[last_row : last_row + span], last_weight),
+        load(11, output_weight_hbm.at[rest:width], output_weight.at[0:span]),
+        load(12, output_weight_hbm.at[last_row : last_row + span], last_weight),
     ]
     if rest > 0:
         output_loads.append(
-            load(14, output_weight_hbm.at[0:rest], output_weight.at[span:width])
+            load(13, output_weight_hbm.at[0:rest], output_weight.at[span:width])
         )
     token_loads[0].start()
 
@@ -164,8 +161,6 @@
         copy.start()
     first_weights.start()
     token_loads[1].start()
-    if rest > 0:
-        other_weights.start()
 
     def normalize(slab):
         hidden = tokens_ref[slab].astype(f32)
@@ -280,6 +275,8 @@
     token_loads[0].wait()
     for copy in small:
         copy.wait()
+    if rest > 0:
+        other_weights.start()
     normalize(slabs[0])
     first_weights.wait()
     first_queries(0)
@@ -299,7 +296,7 @@
     normed_copies[1].start()
     first_queries(1)
     first_copy(1).start()
-    for copy in (cache_weights, stale_load, text_load, keep_load, order_load, count_load):
+    for copy in (cache_weights, stale_load, text_load, keep_load, order_load):
         copy.start()
     for copy in output_loads:
         copy.start()
@@ -345,7 +342,7 @@
             forward(0)
 
 
-    for copy in (stale_load, text_load, keep_load, order_load, count_load):
+    for copy in (stale_load, text_load, keep_load, order_load):
         copy.wait()
 
     keep_row = keep_ref[pl.ds(pl.multiple_of(me * patch, patch), patch)].astype(f32)
@@ -549,7 +546,6 @@
     wide = 512 if full % 512 == 0 else full
     raw_copy = pltpu.make_async_copy(raw, raw_hbm, sems.at[0])
     raw_copy.start()
-    copies = []
     for c in range(full // wide):
         here = slice(c * wide, (c + 1) * wide)
         updated[:, here] = (
@@ -557,12 +553,8 @@
             + modulation[2:3, here]
             * jnp.dot(last[...], last_weight[:, here], preferred_element_type=f32)
         ).astype(bf16)
-        copies.append(
-            pltpu.make_async_copy(updated.at[:, here], updated_hbm.at[:, here], sems.at[1 + c])
-        )
-        copies[c].start()
-    for copy in copies:
-        copy.wait()
+        pltpu.make_async_copy(updated.at[:, here], updated_hbm.at[:, here], sems.at[1]).start()
+    pltpu.make_async_copy(updated, updated_hbm, sems.at[1]).wait()
     raw_copy.wait()
 
 
@@ -601,11 +593,10 @@
             pltpu.VMEM(modulation.shape, f32),
             pltpu.VMEM(stale_cache.shape, bf16),
         ),
-        in_specs=[hbm] * 10,
+        in_specs=[hbm, pl.BlockSpec(memory_space=pltpu.SMEM)] + [hbm] * 8,
         out_specs=(vmem,) * 5,
         scratch_shapes=[
             pltpu.SMEM(patch_order.shape, jnp.int32),
-            pltpu.SMEM(text_count.shape, jnp.int32),
             pltpu.VMEM(video_tokens.shape, bf16),
             pltpu.VMEM(norm_gains.shape, f32),
             pltpu.VMEM(video_keep.shape, jnp.int32),
@@ -634,7 +625,7 @@
             pltpu.VMEM((2, rows, width), bf16),
             pltpu.VMEM((rows, model), bf16),
             pltpu.VMEM((rows, model), bf16),
-            pltpu.SemaphoreType.DMA((15,)),
+            pltpu.SemaphoreType.DMA((14,)),
             pltpu.SemaphoreType.DMA((8,)),
             pltpu.SemaphoreType.DMA((2,)),
             pltpu.SemaphoreType.DMA((2 * pairs + 1,)),
@@ -671,7 +662,7 @@
         out_specs=(hbm, hbm),
         scratch_shapes=[
             pltpu.VMEM(video_tokens.shape, bf16),
-            pltpu.SemaphoreType.DMA((1 + model // (512 if model % 512 == 0 else model),)),
+            pltpu.SemaphoreType.DMA((2,)),
         ],
         compiler_params=pltpu.CompilerParams(vmem_limit_bytes=16 * 1024 * 1024),
     )(*[pltpu.with_memory_space_constraint(array, pltpu.VMEM) for array in handed])

time: 43.2 us -> 43.2 us (level)
  no operation moved by 1% of the time
where the time goes in v4:
time: 43.2 us; the launch traced here: 43 us
  Pallas kernels  41.8 us (97%)
  between operations  1.29 us (3%)
    pallas_call x1, Pallas kernels, on_device(): pl.pallas_call(kernel, out_shape=(pltpu.VMEM(video_tokens.shape, f32), pl...  40.3 us
    pallas_call x1, Pallas kernels, on_device(): pl.pallas_call(finish, out_shape=(jax.ShapeDtypeStruct(video_tokens.shape...  1.43 us

profile of v4, /device:TPU:0, one launch (start us, length us, event | category | flops | bytes accessed | tf_op | source)
XLA Modules:
  0.0 43.0 jit_solution(15681365458340486864)
XLA Ops:
  1.3 40.3 %shard_map.113 = (f32[256,1536]{1,0:T(8,128)S(1)}, bf16[256,256]{1,0:T(8,128)(2,1)S(1)}, bf16[256,1536]{1,0:T(8,128)(2,1)S(1)}, f32[3,1536]{1,0:T(4,128)S(1)}, bf16[2,512,768]{2,1,0:T(8,128)(2,1)S(1)}) custom-call(s32[8]{0:T(128)} %order_hbm.1, s32[1]{0:T(128)S(6)} %copy.12.count_ref, bf16[256,1536]{1,0:T(8,128)(2,1)} %tokens_hbm.1, ...), custom_call_target="tpu_custom_call" | custom-call | tf_op jit(solution)/shard_map/pallas_call | solution.py:587
  41.6 1.4 %shard_map.114 = (bf16[256,1536]{1,0:T(8,128)(2,1)}, bf16[2,512,768]{2,1,0:T(8,128)(2,1)}) custom-call(f32[256,1536]{1,0:T(8,128)S(1)} %get-tuple-element.7.base, bf16[256,256]{1,0:T(8,128)(2,1)S(1)} %get-tuple-element.8.last, bf16[256,1536]{1,0:T(8,128)(2,1)S(1)} %get-tuple-element.9.last_weight, f32[3,1536]{1,0:T(4,128)S(1)} %get-tuple-element.10.modulation, ...), custom_call_target="tpu_custom_call" | custom-call | tf_op jit(solution)/shard_map/pallas_call | solution.py:655
